TPU v7x, 32 devices: a whole 2x2x4 slice. The times are simulated.
32 devices in a mesh: grp: 4 (over x, core), dev: 8 (over z, y).
Axes of the slice: x: 2, y: 2, z: 4, core: 2. Of those that a mesh axis runs over, the one named last changes fastest.
Arguments:
- node_features: float32 [16384, 768], P(('grp', 'dev')), may hold values from -6 to 6
- tiles: bfloat16 [896, 128, 128], P(('grp', 'dev')), may hold values from -0.1875 to 0.1875
- tile_list: int32 [896, 2], replicated, may hold values from 0 to 127, as said below
- weight: float32 [768, 768], replicated, may hold values from -0.21875 to 0.21875
- texts: float32 [1024, 768], P(('grp', 'dev')), may hold values from -6 to 6
- selected: int32 [1024], P(('grp', 'dev')), may hold values from 0 to 16383, as said below
- pairing: int32 [1024], P(('grp', 'dev')), may hold values from 0 to 1023, each once
Outputs:
- contrast_loss: float32 [], replicated
- grad_nodes: float32 [16384, 768], P(('grp', 'dev'))
- grad_weight: float32 [768, 768], replicated
- grad_texts: float32 [1024, 768], P(('grp', 'dev'))
Inputs may be any that keep to these rules, and one draw needn't show every extreme that they name: `tile_list`: device number p = grp index * (devices along dev) + dev index holds node blocks p * 4 to (p + 1) * 4 - 1 and tiles p * 28 to (p + 1) * 28 - 1. A tile's row block lies on the device that holds the tile; its column block lies on that device, on another device of the same grp index, or on the device of the same dev index in another grp. At most 2 tiles of one device have column blocks on any one other device; in every draw each device has one other device of its grp index and one of its dev index at that most. `selected`: distinct ids; the ids listed on a device are nodes of that device.
All inputs are finite; a program needn't handle non-finite values.
Results may differ from a plain program's by a relative error of at most 0.0004.
The roundings to bfloat16 on the way count: a program that leaves them out, or rounds other values in their place, can miss the bound.
Values may be sent and summed in bfloat16 or wider, within the bound.
No kernel may reach another device: no remote copies, remote signals or barrier semaphores. Data moves between devices by JAX's collectives and lax.ppermute only.
A program may use at most 128 MiB of HBM per device.

v0:
```python
import jax
import jax.numpy as jnp
from jax import lax
from jax.sharding import PartitionSpec as P

CAP = 2
SCALE = 1.0 / 0.07
EPS = 1e-06
PRECISE = lax.Precision.HIGHEST
ROOT_HALF = 0.7071067811865476
INV_ROOT_TWO_PI = 0.3989422804014327


def gelu_value(value):
    return 0.5 * value * (1.0 + lax.erf(value * ROOT_HALF))


def gelu_slope(value):
    return (
        0.5 * (1.0 + lax.erf(value * ROOT_HALF))
        + value * jnp.exp(-0.5 * value * value) * INV_ROOT_TWO_PI
    )


def slot_plan(peer_lists, peer_ids, device, blocks_dev, capacity):
    col_owner = peer_lists[:, :, 1] // blocks_dev
    wanted = (col_owner == device) & (peer_ids[:, None] != device)
    slot_order = jnp.cumsum(wanted.astype(jnp.int32), axis=1) - 1
    local_block = peer_lists[:, :, 1] - device * blocks_dev
    slot_hits = wanted[:, :, None] & (
        slot_order[:, :, None] == jnp.arange(capacity, dtype=jnp.int32)[None, None, :]
    )
    block_index = jnp.sum(jnp.where(slot_hits, local_block[:, :, None], 0), axis=1)
    slot_valid = jnp.any(slot_hits, axis=1)
    return (block_index.reshape(-1), slot_valid.reshape(-1))


def slot_pick(slot_of_tile, keep, slots_all):
    return (slot_of_tile[None, :] == jnp.arange(slots_all, dtype=jnp.int32)[:, None]) & keep[
        None, :
    ]


def land_blocks(total, block_index, valid, incoming):
    return total.at[block_index].add(jnp.where(valid[:, None, None], incoming, 0.0))


def shards(node_features, tiles, tile_list, weight, texts, selected, pairing):
    groups = lax.axis_size("grp")
    members = lax.axis_size("dev")
    grp_index = lax.axis_index("grp")
    dev_index = lax.axis_index("dev")
    device = grp_index * members + dev_index
    block_rows = tiles.shape[1]
    feat_width = node_features.shape[1]
    blocks_dev = node_features.shape[0] // block_rows
    tile_dev = tiles.shape[0]
    sel_dev = selected.shape[0]
    capacity = CAP
    total_sel = sel_dev * groups * members
    rounded = node_features.astype(jnp.bfloat16).reshape(blocks_dev, block_rows, feat_width)
    my_list = lax.dynamic_slice_in_dim(tile_list, device * tile_dev, tile_dev, 0)
    row_block = my_list[:, 0] - device * blocks_dev
    col_owner = my_list[:, 1] // blocks_dev
    col_block = my_list[:, 1] - col_owner * blocks_dev
    owner_grp = col_owner // members
    owner_dev = col_owner % members
    is_local = col_owner == device
    is_near = (owner_grp == grp_index) & jnp.logical_not(is_local)
    is_far = (owner_dev == dev_index) & (owner_grp != grp_index)
    positions = jnp.arange(tile_dev, dtype=jnp.int32)
    earlier = (col_owner[:, None] == col_owner[None, :]) & (positions[None, :] < positions[:, None])
    slot_rank = jnp.sum(earlier.astype(jnp.int32), axis=1)
    near_slot = owner_dev * capacity + slot_rank
    far_slot = owner_grp * capacity + slot_rank
    group_lists = lax.dynamic_slice_in_dim(
        tile_list, grp_index * members * tile_dev, members * tile_dev, 0
    ).reshape(members, tile_dev, 2)
    near_peers = grp_index * members + jnp.arange(members, dtype=jnp.int32)
    near_index, near_valid = slot_plan(group_lists, near_peers, device, blocks_dev, capacity)
    far_lists = lax.dynamic_index_in_dim(
        tile_list.reshape(groups, members, tile_dev, 2), dev_index, 1, False
    )
    far_peers = jnp.arange(groups, dtype=jnp.int32) * members + dev_index
    far_index, far_valid = slot_plan(far_lists, far_peers, device, blocks_dev, capacity)
    zero_half = jnp.zeros((), jnp.bfloat16)
    sel_local = selected - device * blocks_dev * block_rows
    sel_block = sel_local // block_rows
    sel_offset = sel_local % block_rows
    picked = jnp.take(tiles, sel_offset, axis=1)
    tile_rows = jnp.where((row_block[:, None] == sel_block[None, :])[:, :, None], picked, zero_half)
    near_pick = slot_pick(near_slot, is_near, members * capacity)
    far_pick = slot_pick(far_slot, is_far, groups * capacity)
    near_rows = jnp.einsum(
        "st,tkc->skc", near_pick.astype(jnp.bfloat16), tile_rows, preferred_element_type=jnp.float32
    ).astype(jnp.bfloat16)
    far_rows = jnp.einsum(
        "st,tkc->skc", far_pick.astype(jnp.bfloat16), tile_rows, preferred_element_type=jnp.float32
    ).astype(jnp.bfloat16)
    local_tile_rows = jnp.where(is_local[:, None, None], tile_rows, zero_half)
    near_send = jnp.where(
        near_valid[:, None, None], jnp.take(rounded, near_index, axis=0), zero_half
    )
    near_blocks = lax.all_to_all(
        near_send.reshape(members, capacity, block_rows, feat_width),
        "dev",
        split_axis=0,
        concat_axis=0,
        tiled=True,
    )
    far_send = jnp.where(far_valid[:, None, None], jnp.take(rounded, far_index, axis=0), zero_half)
    far_blocks = lax.all_to_all(
        far_send.reshape(groups, capacity, block_rows, feat_width),
        "grp",
        split_axis=0,
        concat_axis=0,
        tiled=True,
    )
    source_table = jnp.concatenate(
        [
            rounded,
            near_blocks.reshape(-1, block_rows, feat_width),
            far_blocks.reshape(-1, block_rows, feat_width),
        ],
        axis=0,
    )
    source_index = jnp.where(
        is_local,
        col_block,
        jnp.where(is_near, blocks_dev + near_slot, blocks_dev + members * capacity + far_slot),
    )
    sources = jnp.take(source_table, source_index, axis=0)
    messages = jnp.einsum("tkc,tcd->kd", tile_rows, sources, preferred_element_type=jnp.float32)
    chosen = node_features[sel_local] + messages
    before = jnp.dot(chosen, weight, precision=PRECISE)
    hidden = gelu_value(before)
    node_norm = jnp.sqrt(jnp.sum(hidden * hidden, axis=1, keepdims=True) + EPS)
    unit_nodes = hidden / node_norm
    text_norm = jnp.sqrt(jnp.sum(texts * texts, axis=1, keepdims=True) + EPS)
    unit_texts = texts / text_norm
    node_rows, pair_rows = (
        lax.all_gather(unit_nodes, "dev", axis=0, tiled=True),
        lax.all_gather(pairing, "dev", axis=0, tiled=True),
    )
    text_cols = lax.all_gather(unit_texts, "grp", axis=0, tiled=True)
    scores = SCALE * lax.dot_general(
        node_rows, text_cols, (((1,), (1,)), ((), ())), precision=PRECISE
    )
    exp_scores = jnp.exp(scores)
    row_total = lax.psum(jnp.sum(exp_scores, axis=1), "dev")
    col_total = lax.psum(jnp.sum(exp_scores, axis=0), "grp")
    col_global = (
        (jnp.arange(groups, dtype=jnp.int32)[:, None] * members + dev_index) * sel_dev
        + jnp.arange(sel_dev, dtype=jnp.int32)[None, :]
    ).reshape(-1)
    target = pair_rows[:, None] == col_global[None, :]
    score_grads = 0.5 * (
        exp_scores / row_total[:, None] + exp_scores / col_total[None, :]
    ) - target.astype(jnp.float32)
    node_part = SCALE * jnp.dot(score_grads, text_cols, precision=PRECISE)
    node_dir = lax.psum_scatter(node_part, "dev", scatter_dimension=0, tiled=True)
    text_part = SCALE * lax.dot_general(
        score_grads, node_rows, (((0,), (0,)), ((), ())), precision=PRECISE
    )
    text_dir = lax.psum_scatter(text_part, "grp", scatter_dimension=0, tiled=True)
    own_rows = lax.dynamic_slice_in_dim(row_total, dev_index * sel_dev, sel_dev, 0)
    own_cols = lax.dynamic_slice_in_dim(col_total, grp_index * sel_dev, sel_dev, 0)
    positive = jnp.sum(jnp.where(target, scores, 0.0))
    lse_sum, pos_sum = lax.psum(
        (jnp.sum(jnp.log(own_rows)) + jnp.sum(jnp.log(own_cols)), positive), ("grp", "dev")
    )
    contrast_loss = lse_sum / (2.0 * total_sel) - pos_sum / total_sel
    node_back = (
        node_dir - unit_nodes * jnp.sum(unit_nodes * node_dir, axis=1, keepdims=True)
    ) / node_norm
    grad_texts = (
        text_dir - unit_texts * jnp.sum(unit_texts * text_dir, axis=1, keepdims=True)
    ) / text_norm
    pre_grad = node_back * gelu_slope(before)
    weight_term = lax.dot_general(chosen, pre_grad, (((0,), (0,)), ((), ())), precision=PRECISE)
    grad_weight = lax.psum(weight_term, ("grp", "dev"))
    row_grads = lax.dot_general(pre_grad, weight, (((1,), (1,)), ((), ())), precision=PRECISE)
    rounded_grads = row_grads.astype(jnp.bfloat16)
    empty_blocks = jnp.zeros((blocks_dev, block_rows, feat_width), jnp.float32)
    local_spread = jnp.einsum(
        "tkc,kd->tcd", local_tile_rows, rounded_grads, preferred_element_type=jnp.float32
    )
    grad_blocks = empty_blocks.at[col_block].add(local_spread)
    near_rows_in = lax.all_to_all(
        near_rows.reshape(members, capacity, sel_dev, block_rows),
        "dev",
        split_axis=0,
        concat_axis=0,
        tiled=True,
    )
    near_grads_in = lax.all_gather(rounded_grads, "dev", axis=0, tiled=True).reshape(
        members, sel_dev, feat_width
    )
    near_spread = jnp.einsum(
        "pqkc,pkd->pqcd", near_rows_in, near_grads_in, preferred_element_type=jnp.float32
    )
    grad_blocks = land_blocks(
        grad_blocks, near_index, near_valid, near_spread.reshape(-1, block_rows, feat_width)
    )
    far_rows_in = lax.all_to_all(
        far_rows.reshape(groups, capacity, sel_dev, block_rows),
        "grp",
        split_axis=0,
        concat_axis=0,
        tiled=True,
    )
    far_grads_in = lax.all_gather(rounded_grads, "grp", axis=0, tiled=True).reshape(
        groups, sel_dev, feat_width
    )
    far_spread = jnp.einsum(
        "pqkc,pkd->pqcd", far_rows_in, far_grads_in, preferred_element_type=jnp.float32
    )
    grad_blocks = land_blocks(
        grad_blocks, far_index, far_valid, far_spread.reshape(-1, block_rows, feat_width)
    )
    grad_nodes = grad_blocks.reshape(-1, feat_width).at[sel_local].add(row_grads)
    return (contrast_loss, grad_nodes, grad_weight, grad_texts)


def solution(mesh):
    return jax.shard_map(
        shards,
        mesh=mesh,
        in_specs=(
            P(("grp", "dev"), None),
            P(("grp", "dev"), None, None),
            P(),
            P(),
            P(("grp", "dev"), None),
            P(("grp", "dev")),
            P(("grp", "dev")),
        ),
        out_specs=(P(), P(("grp", "dev"), None), P(), P(("grp", "dev"), None)),
        check_vma=False,
    )
```

profile of v0, /device:TPU:0, one launch (start us, length us, event | category | flops | bytes accessed | tf_op | source)
XLA Modules:
  0.0 443.1 jit_solution(16403538620831499144)
XLA Ops:
  7.2 0.9 reshape.393
  8.9 1.5 convert_element_type.25
  10.7 1.8 gather_fusion.3
  12.5 2.8 select_select_fusion.1
  15.3 4.4 all-to-all-start.1
  19.7 0.8 constant_dynamic-slice_fusion.1
  21.1 2.5 gather_fusion.2
  23.9 4.0 select_select_fusion
  27.9 12.5 %all-to-all-done.1 = bf16[4,2,128,768]{3,2,1,0:T(8,128)(2,1)} async-done(((bf16[4,2,128,768]{3,2,1,0:T(8,128)(2,1)}), bf16[4,2,128,768]{3,2,1,0:T(8,128)(2,1)}, u32[]{:S(2)}, u32[]{:S(2)}) %all-to-all-start.1) | async-done | bytes 1572896 | tf_op jit(solution)/shard_map/all_to_all | solution.py:112
  40.4 6.6 %all-to-all-start = ((bf16[8,2,128,768]{3,2,1,0:T(8,128)(2,1)}), bf16[8,2,128,768]{3,2,1,0:T(8,128)(2,1)}, u32[]{:S(2)}, u32[]{:S(2)}) async-start(bf16[8,2,128,768]{3,2,1,0:T(8,128)(2,1)} %select_select_fusion), calls=%async_computation | async-start | bytes 6291456 | tf_op jit(solution)/shard_map/all_to_all | solution.py:104
  47.3 2.1 gather_fusion
  50.7 2.8 gather_fusion.1
  53.7 64.1 %all-reduce = s32[256]{0:T(256)S(1)} all-reduce(s32[256]{0:T(256)S(1)} %dynamic-update-slice), channel_id=1, replica_groups=mesh['grp'=4,'dev'=8] {'dev'}, use_global_device_ids=true, to_apply=%add | all-reduce | flops 256 | bytes 2048
  117.7 0.8 constant_dynamic-slice_fusion.2
  119.0 6.6 %all_gather.16 = f32[128,768]{1,0:T(8,128)} all-gather(f32[32,768]{1,0:T(8,128)S(1)} %broadcast_divide_fusion), channel_id=1, replica_groups=mesh['grp'=4,'dev'=8] {'grp'}, dimensions={0}, use_global_device_ids=true | all-gather | bytes 491520 | tf_op jit(solution)/shard_map/all_gather | solution.py:145
  125.6 1.1 bitcast_select_fusion.2
  126.8 5.8 %pad_maximum_fusion = bf16[28,128,768]{2,1,0:T(8,128)(2,1)} fusion(bf16[8,128,768]{2,1,0:T(8,128)(2,1)} %bitcast.17, bf16[16,128,768]{2,1,0:T(8,128)(2,1)} %bitcast.11, bf16[4,128,768]{2,1,0:T(8,128)(2,1)S(1)} %bitcast.101), kind=kLoop, calls=%fused_computation.10 | loop fusion | flops 5505024 | bytes 11010048 | tf_op jit(solution)/shard_map/concatenate | solution.py:119
  132.6 6.0 %gather_fusion.4 = bf16[28,128,768]{2,1,0:T(8,128)(2,1)} fusion(bf16[28,128,768]{2,1,0:T(8,128)(2,1)} %pad_maximum_fusion, s32[1024]{0:T(1024)S(1)} %pad_clamp_fusion), kind=kCustom, calls=%fused_computation.4 | custom fusion | bytes 11010160 | tf_op jit(solution)/shard_map/jit(_take)/gather | solution.py:132
  138.6 3.6 fusion.7
  142.2 1.5 multiply_reduce_fusion.3
  143.9 32.1 %all_gather.15 = f32[256,768]{1,0:T(8,128)S(1)} all-gather(f32[32,768]{1,0:T(8,128)S(1)} %broadcast_divide_fusion.1), channel_id=1, replica_groups=mesh['grp'=4,'dev'=8] {'dev'}, dimensions={0}, use_global_device_ids=true | all-gather | bytes 884736 | tf_op jit(solution)/shard_map/all_gather | solution.py:142
  176.0 2.0 fusion.15
  178.0 19.6 %psum.35 = f32[256]{0:T(256)S(1)} all-reduce(f32[256]{0:T(256)S(1)} %get-tuple-element.6), channel_id=1, replica_groups=mesh['grp'=4,'dev'=8] {'dev'}, use_global_device_ids=true, to_apply=%region_10.11 | all-reduce | flops 256 | bytes 2048 | tf_op jit(solution)/shard_map/psum | solution.py:150
  197.6 5.6 %psum.36 = f32[128]{0:T(128)S(1)} all-reduce(f32[128]{0:T(128)S(1)} %get-tuple-element.5), channel_id=1, replica_groups=mesh['grp'=4,'dev'=8] {'grp'}, use_global_device_ids=true, to_apply=%region_13.14 | all-reduce | flops 128 | bytes 1024 | tf_op jit(solution)/shard_map/psum | solution.py:151
  203.3 2.3 convolution_multiply_fusion.1
  205.7 2.8 convolution_multiply_fusion
  209.4 3.4 all-to-all-start.2
  216.5 40.7 %all-reduce.1 = (f32[]{:T(128)}, f32[]{:T(128)}) all-reduce(f32[]{:T(128)S(6)} %add.310, f32[]{:T(128)} %get-tuple-element.4), channel_id=1, replica_groups=mesh['grp'=4,'dev'=8] {'grp','dev'}, use_global_device_ids=true, to_apply=%region_15.16 | all-reduce | flops 2 | bytes 16 | tf_op jit(solution)/shard_map/psum | solution.py:169
  258.5 1.1 multiply_reduce_fusion
  259.6 1.6 subtract_divide_fusion
  261.2 29.5 %reduce-scatter.3.cloned.1.call-done = f32[32,768]{1,0:T(8,128)} async-done(((f32[256,768]{1,0:T(8,128)}), f32[32,768]{1,0:T(8,128)}) %reduce-scatter.3.cloned.1.call-update) | async-done | bytes 98320 | tf_op jit(solution)/shard_map/reduce_scatter | solution.py:161
  290.7 1.2 multiply_reduce_fusion.1
  291.9 4.4 fusion.57
  296.3 2.3 fusion.63
  298.5 6.1 %fusion.12 = f32[28,128,768]{2,1,0:T(8,128)} fusion(bf16[28,32,128]{2,1,0:T(8,128)(2,1)S(1)} %bitcast_select_fusion.2, pred[28]{0:T(512)(128)(4,1)S(1)} %get-tuple-element.14, bf16[32,768]{1,0:T(8,128)(2,1)S(1)} %get-tuple-element.34), kind=kOutput, calls=%fused_computation.28 | convolution fusion | flops 176275456 | bytes 11288604 | tf_op jit(solution)/shard_map/tkc,kd->tcd/dot_general | solution.py:185
  304.6 1.3 broadcast_in_dim.214
  305.9 25.5 %scatter_fusion = f32[4,128,768]{2,1,0:T(8,128)} fusion(f32[4,128,768]{2,1,0:T(8,128)} %broadcast_in_dim.214, s32[28]{0:T(128)S(1)} %get-tuple-element.15, f32[28,128,768]{2,1,0:T(8,128)} %fusion.12), kind=kCustom, calls=%fused_computation.5 | custom fusion | flops 2752512 | bytes 33030256 | tf_op jit(solution)/shard_map/scatter-add | solution.py:188
  331.4 31.2 %all_gather.18 = bf16[256,768]{1,0:T(8,128)(2,1)S(1)} all-gather(bf16[32,768]{1,0:T(8,128)(2,1)S(1)} %get-tuple-element.34), channel_id=1, replica_groups=mesh['grp'=4,'dev'=8] {'dev'}, dimensions={0}, use_global_device_ids=true | all-gather | bytes 442368 | tf_op jit(solution)/shard_map/all_gather | solution.py:196
  362.5 3.3 all-to-all-start.3
  365.8 1.0 fusion.64
  366.8 3.4 bitcast_select_fusion
  370.2 14.5 %scatter_fusion.1 = f32[4,128,768]{2,1,0:T(8,128)} fusion(f32[4,128,768]{2,1,0:T(8,128)} %scatter_fusion, s32[16]{0:T(128)S(1)} %fusion.47, f32[16,128,768]{2,1,0:T(8,128)} %bitcast_select_fusion), kind=kCustom, calls=%fused_computation.6 | custom fusion | flops 1572864 | bytes 18874432 | tf_op jit(solution)/shard_map/scatter-add | solution.py:45
  384.8 5.8 %all_gather.19 = bf16[128,768]{1,0:T(8,128)(2,1)S(1)} all-gather(bf16[32,768]{1,0:T(8,128)(2,1)S(1)} %get-tuple-element.34), channel_id=1, replica_groups=mesh['grp'=4,'dev'=8] {'grp'}, dimensions={0}, use_global_device_ids=true | all-gather | bytes 245760 | tf_op jit(solution)/shard_map/all_gather | solution.py:212
  391.2 2.0 bitcast_select_fusion.1
  393.2 7.4 %scatter_fusion.2 = f32[4,128,768]{2,1,0:T(8,128)} fusion(f32[4,128,768]{2,1,0:T(8,128)} %scatter_fusion.1, s32[8]{0:T(128)S(1)} %fusion.48, f32[8,128,768]{2,1,0:T(8,128)} %bitcast_select_fusion.1), kind=kCustom, calls=%fused_computation.7 | custom fusion | flops 786432 | bytes 9437216 | tf_op jit(solution)/shard_map/scatter-add | solution.py:45
  400.7 3.4 scatter_fusion.3
  404.1 28.1 %all-reduce.4.cloned.1.call-done = f32[768,768]{1,0:T(8,128)} async-done(((f32[768,768]{1,0:T(8,128)}), f32[768,768]{1,0:T(8,128)}) %all-reduce.4.cloned.1.call-update) | async-done | bytes 2359312 | tf_op jit(solution)/shard_map/psum | solution.py:181
  432.2 3.2 copy.43
  (94 shorter events, 7.8 us)
Async XLA Ops:
  7.2 135.0 %copy-start = (f32[768,768]{1,0:T(8,128)S(1)}, f32[768,768]{1,0:T(8,128)}, u32[]{:S(2)}) copy-start(f32[768,768]{1,0:T(8,128)} %param.10) | copy-start | bytes 7077892
  15.3 25.1 %all-to-all-start.1 = ((bf16[4,2,128,768]{3,2,1,0:T(8,128)(2,1)}), bf16[4,2,128,768]{3,2,1,0:T(8,128)(2,1)}, u32[]{:S(2)}, u32[]{:S(2)}) async-start(bf16[4,2,128,768]{3,2,1,0:T(8,128)(2,1)} %select_select_fusion.1), calls=%async_computation.1 | async-start | bytes 3145728 | tf_op jit(solution)/shard_map/all_to_all | solution.py:112
  27.9 19.4 %copy-start.8 = (s32[32]{0:T(128)S(1)}, s32[32]{0:T(128)}, u32[]{:S(2)}) copy-start(s32[32]{0:T(128)} %param.12) | copy-start | bytes 388
  27.9 21.5 %copy-start.10 = (u32[32]{0:T(128)S(1)}, u32[32]{0:T(128)}, u32[]{:S(2)}) copy-start(u32[32]{0:T(128)} %constant.215) | copy-start | bytes 388
  27.9 25.5 %copy-start.9 = (s32[32]{0:T(128)S(1)}, s32[32]{0:T(128)}, u32[]{:S(2)}) copy-start(s32[32]{0:T(128)} %param.13) | copy-start | bytes 388
  27.9 90.8 %copy-start.3 = (f32[32,768]{1,0:T(8,128)S(1)}, f32[32,768]{1,0:T(8,128)}, u32[]{:S(2)}) copy-start(f32[32,768]{1,0:T(8,128)} %param.11) | copy-start | bytes 294916
  40.4 86.4 %all-to-all-start = ((bf16[8,2,128,768]{3,2,1,0:T(8,128)(2,1)}), bf16[8,2,128,768]{3,2,1,0:T(8,128)(2,1)}, u32[]{:S(2)}, u32[]{:S(2)}) async-start(bf16[8,2,128,768]{3,2,1,0:T(8,128)(2,1)} %select_select_fusion), calls=%async_computation | async-start | bytes 6291456 | tf_op jit(solution)/shard_map/all_to_all | solution.py:104
  47.1 211.4 %reduce-scatter.5.cloned.1.call-start = ((), (), s32[]{:S(2)}) async-start(), calls=%async_computation.8 | async-start | bytes 491520 | tf_op jit(solution)/shard_map/reduce_scatter | solution.py:165
  142.2 35.8 %copy-start.6 = (f32[32,768]{1,0:T(8,128)}, f32[32,768]{1,0:T(8,128)S(1)}, u32[]{:S(2)}) copy-start(f32[32,768]{1,0:T(8,128)S(1)} %fusion.7) | copy-start | bytes 294916
  142.2 33.8 %copy-start.2 = (f32[128,768]{1,0:T(8,128)S(1)}, f32[128,768]{1,0:T(8,128)}, u32[]{:S(2)}) copy-start(f32[128,768]{1,0:T(8,128)} %all_gather.16) | copy-start | bytes 1179652
  205.6 52.9 %copy-start.4 = (f32[32,768]{1,0:T(8,128)S(1)}, f32[32,768]{1,0:T(8,128)}, u32[]{:S(2)}) copy-start(f32[32,768]{1,0:T(8,128)} %param.11) | copy-start | bytes 294916
  205.6 86.2 %copy-start.7 = (f32[32,768]{1,0:T(8,128)S(1)}, f32[32,768]{1,0:T(8,128)}, u32[]{:S(2)}) copy-start(f32[32,768]{1,0:T(8,128)} %copy-done.6) | copy-start | bytes 294916
  205.6 85.1 %reduce-scatter.3.cloned.1.call-start = ((), (), s32[]{:S(2)}) async-start(), calls=%async_computation.6 | async-start | bytes 884736 | tf_op jit(solution)/shard_map/reduce_scatter | solution.py:161
  209.4 153.1 %all-to-all-start.2 = ((bf16[8,2,32,128]{3,2,1,0:T(8,128)(2,1)}), bf16[8,2,32,128]{3,2,1,0:T(8,128)(2,1)S(1)}, u32[]{:S(2)}, u32[]{:S(2)}) async-start(bf16[8,2,32,128]{3,2,1,0:T(8,128)(2,1)} %copy.27), calls=%async_computation.3 | async-start | bytes 262144 | tf_op jit(solution)/shard_map/all_to_all | solution.py:189
  212.8 219.4 %all-reduce.4.cloned.1.call-start = ((), (), s32[]{:S(2)}) async-start(), calls=%async_computation.7 | async-start | bytes 4718592 | tf_op jit(solution)/shard_map/psum | solution.py:181
  290.7 5.6 %copy-start.5 = (f32[32,768]{1,0:T(8,128)S(1)}, f32[32,768]{1,0:T(8,128)}, u32[]{:S(2)}) copy-start(f32[32,768]{1,0:T(8,128)} %reduce-scatter.3.cloned.1.call-done) | copy-start | bytes 294916
  362.5 28.0 %all-to-all-start.3 = ((bf16[4,2,32,128]{3,2,1,0:T(8,128)(2,1)}), bf16[4,2,32,128]{3,2,1,0:T(8,128)(2,1)S(1)}, u32[]{:S(2)}, u32[]{:S(2)}) async-start(bf16[4,2,32,128]{3,2,1,0:T(8,128)(2,1)} %copy.30), calls=%async_computation.4 | async-start | bytes 131072 | tf_op jit(solution)/shard_map/all_to_all | solution.py:205
  400.7 34.8 %copy-start.1 = (f32[768,768]{1,0:T(8,128)S(1)}, f32[768,768]{1,0:T(8,128)}, u32[]{:S(2)}) copy-start(f32[768,768]{1,0:T(8,128)} %param.10) | copy-start | bytes 7077892
Sparse Core Ops, SparseCore 0:
  205.7 17.4 reduce-scatter.4
  227.1 63.5 reduce-scatter.2
  296.8 135.3 all-reduce.3
where the time goes:
time: 445 us; the launch traced here: 443 us
  blocking collectives  206 us (46%)
  other arithmetic  78.7 us (18%)
  waiting for transfers between devices  70.1 us (16%)
  matrix products  27 us (6%)
  local copies, waits for them, and re-layouts  25.3 us (6%)
  between operations  18.5 us (4%)
  starting transfers between devices  17.8 us (4%)
    unnamed x1, blocking collectives  64.1 us
    psum x1, blocking collectives, shards(): lax.psum((jnp.sum(jnp.log(own_rows)) + jnp.sum(jnp.log(own_cols)), positi...  40.7 us
    all_gather x1, blocking collectives, shards(): lax.all_gather(unit_nodes, 'dev', axis=0, tiled=True)  32.1 us
    all_gather x1, blocking collectives, shards(): lax.all_gather(rounded_grads, 'dev', axis=0, tiled=True)  31.2 us
    reduce_scatter x1, waiting for transfers between devices, shards(): lax.psum_scatter(node_part, 'dev', scatter_dimension=0, tiled=True)  29.5 us
    psum x1, waiting for transfers between devices, shards(): grad_weight = lax.psum(weight_term, ('grp', 'dev'))  28.1 us
    scatter-add x1, other arithmetic, shards(): grad_blocks = empty_blocks.at[col_block].add(local_spread)  25.5 us
    scatter-add x2, other arithmetic, land_blocks(): total.at[block_index].add(jnp.where(valid[:, None, None], incoming, 0.0))  22 us
  transfers between devices with their start and end apart: 7, of which 3 were waited for; matrix products, arithmetic and copies ran while one was open for 22% of the time, Pallas kernels for 0%

commit v1 on v0

--- a/solution.py
+++ b/solution.py
@@ -2,6 +2,7 @@
 import jax.numpy as jnp
 from jax import lax
 from jax.sharding import PartitionSpec as P
+from jax.lax import psum
 
 CAP = 2
 SCALE = 1.0 / 0.07
@@ -178,7 +179,8 @@
     ) / text_norm
     pre_grad = node_back * gelu_slope(before)
     weight_term = lax.dot_general(chosen, pre_grad, (((0,), (0,)), ((), ())), precision=PRECISE)
-    grad_weight = lax.psum(weight_term, ("grp", "dev"))
+    save_islands = lambda buf, lane_axis, axis_key: psum(psum(buf, axis_name=lane_axis), axis_key)
+    grad_weight = save_islands(weight_term, "dev", "grp")
     row_grads = lax.dot_general(pre_grad, weight, (((1,), (1,)), ((), ())), precision=PRECISE)
     rounded_grads = row_grads.astype(jnp.bfloat16)
     empty_blocks = jnp.zeros((blocks_dev, block_rows, feat_width), jnp.float32)

time: 445 us -> 475 us (1.067)
  waiting for transfers between devices: 70.1 us -> 88.6 us
    reduce_scatter x1, waiting for transfers between devices: 29.5 us -> 57.5 us  [shards(): lax.psum_scatter(node_part, 'dev', scatter_dimension=0, tiled=True)]
    psum x1 -> x2, waiting for transfers between devices: 28.1 us -> 18.5 us  [the longest x1 17 us: shards(): psum(psum(buf, axis_name=lane_axis), axis_key)]
  transfers between devices with their start and end apart: 7 -> 8, of which waited for: 3 -> 4; matrix products, arithmetic and copies ran while one was open for 22% -> 22% of each run, Pallas kernels for 0% -> 0%
where the time goes in v1:
time: 475 us; the launch traced here: 473 us
  blocking collectives  210 us (44%)
  waiting for transfers between devices  88.6 us (19%)
  other arithmetic  81.8 us (17%)
  matrix products  29.8 us (6%)
  local copies, waits for them, and re-layouts  25.3 us (5%)
  starting transfers between devices  18.7 us (4%)
  between operations  18.5 us (4%)
    unnamed x1, blocking collectives  64.1 us
    reduce_scatter x1, waiting for transfers between devices, shards(): lax.psum_scatter(node_part, 'dev', scatter_dimension=0, tiled=True)  57.5 us
    psum x1, blocking collectives, shards(): lax.psum((jnp.sum(jnp.log(own_rows)) + jnp.sum(jnp.log(own_cols)), positi...  43 us
    all_gather x1, blocking collectives, shards(): lax.all_gather(rounded_grads, 'dev', axis=0, tiled=True)  32.4 us
    all_gather x1, blocking collectives, shards(): lax.all_gather(unit_nodes, 'dev', axis=0, tiled=True)  32.1 us
    scatter-add x1, other arithmetic, shards(): grad_blocks = empty_blocks.at[col_block].add(local_spread)  25.4 us
    scatter-add x2, other arithmetic, land_blocks(): total.at[block_index].add(jnp.where(valid[:, None, None], incoming, 0.0))  22.4 us
    psum x1, blocking collectives, shards(): row_total = lax.psum(jnp.sum(exp_scores, axis=1), 'dev')  19.6 us
  transfers between devices with their start and end apart: 8, of which 4 were waited for; matrix products, arithmetic and copies ran while one was open for 22% of the time, Pallas kernels for 0%

profile of v1, /device:TPU:0, one launch (start us, length us, event | category | flops | bytes accessed | tf_op | source)
XLA Modules:
  0.0 473.2 jit_solution(13719974545332323516)
XLA Ops:
  7.2 0.9 reshape.393
  8.9 1.5 convert_element_type.25
  10.7 1.8 gather_fusion.3
  12.5 2.8 select_select_fusion.1
  15.3 4.4 all-to-all-start.1
  19.7 0.8 constant_dynamic-slice_fusion.1
  21.1 2.5 gather_fusion.2
  23.9 4.0 select_select_fusion
  27.9 12.5 %all-to-all-done.1 = bf16[4,2,128,768]{3,2,1,0:T(8,128)(2,1)} async-done(((bf16[4,2,128,768]{3,2,1,0:T(8,128)(2,1)}), bf16[4,2,128,768]{3,2,1,0:T(8,128)(2,1)}, u32[]{:S(2)}, u32[]{:S(2)}) %all-to-all-start.1) | async-done | bytes 1572896 | tf_op jit(solution)/shard_map/all_to_all | solution.py:113
  40.4 6.6 %all-to-all-start = ((bf16[8,2,128,768]{3,2,1,0:T(8,128)(2,1)}), bf16[8,2,128,768]{3,2,1,0:T(8,128)(2,1)}, u32[]{:S(2)}, u32[]{:S(2)}) async-start(bf16[8,2,128,768]{3,2,1,0:T(8,128)(2,1)} %select_select_fusion), calls=%async_computation | async-start | bytes 6291456 | tf_op jit(solution)/shard_map/all_to_all | solution.py:105
  47.3 2.1 gather_fusion
  50.7 2.8 gather_fusion.1
  53.7 64.1 %all-reduce = s32[256]{0:T(256)S(1)} all-reduce(s32[256]{0:T(256)S(1)} %dynamic-update-slice), channel_id=1, replica_groups=mesh['grp'=4,'dev'=8] {'dev'}, use_global_device_ids=true, to_apply=%add | all-reduce | flops 256 | bytes 2048
  119.0 6.6 %all_gather.16 = f32[128,768]{1,0:T(8,128)} all-gather(f32[32,768]{1,0:T(8,128)S(1)} %broadcast_divide_fusion), channel_id=1, replica_groups=mesh['grp'=4,'dev'=8] {'grp'}, dimensions={0}, use_global_device_ids=true | all-gather | bytes 491520 | tf_op jit(solution)/shard_map/all_gather | solution.py:146
  125.6 1.1 bitcast_select_fusion.2
  126.8 5.8 %pad_maximum_fusion = bf16[28,128,768]{2,1,0:T(8,128)(2,1)} fusion(bf16[8,128,768]{2,1,0:T(8,128)(2,1)} %bitcast.17, bf16[16,128,768]{2,1,0:T(8,128)(2,1)} %bitcast.11, bf16[4,128,768]{2,1,0:T(8,128)(2,1)S(1)} %bitcast.101), kind=kLoop, calls=%fused_computation.10 | loop fusion | flops 5505024 | bytes 11010048 | tf_op jit(solution)/shard_map/concatenate | solution.py:120
  132.6 6.0 %gather_fusion.4 = bf16[28,128,768]{2,1,0:T(8,128)(2,1)} fusion(bf16[28,128,768]{2,1,0:T(8,128)(2,1)} %pad_maximum_fusion, s32[1024]{0:T(1024)S(1)} %pad_clamp_fusion), kind=kCustom, calls=%fused_computation.4 | custom fusion | bytes 11010160 | tf_op jit(solution)/shard_map/jit(_take)/gather | solution.py:133
  138.6 3.6 fusion.7
  142.2 1.5 multiply_reduce_fusion.3
  143.9 32.1 %all_gather.15 = f32[256,768]{1,0:T(8,128)S(1)} all-gather(f32[32,768]{1,0:T(8,128)S(1)} %broadcast_divide_fusion.1), channel_id=1, replica_groups=mesh['grp'=4,'dev'=8] {'dev'}, dimensions={0}, use_global_device_ids=true | all-gather | bytes 884736 | tf_op jit(solution)/shard_map/all_gather | solution.py:143
  176.0 2.0 fusion.15
  178.0 19.6 %psum.42 = f32[256]{0:T(256)S(1)} all-reduce(f32[256]{0:T(256)S(1)} %get-tuple-element.6), channel_id=1, replica_groups=mesh['grp'=4,'dev'=8] {'dev'}, use_global_device_ids=true, to_apply=%region_10.11 | all-reduce | flops 256 | bytes 2048 | tf_op jit(solution)/shard_map/psum | solution.py:151
  197.7 5.6 %psum.43 = f32[128]{0:T(128)S(1)} all-reduce(f32[128]{0:T(128)S(1)} %get-tuple-element.5), channel_id=1, replica_groups=mesh['grp'=4,'dev'=8] {'grp'}, use_global_device_ids=true, to_apply=%region_13.14 | all-reduce | flops 128 | bytes 1024 | tf_op jit(solution)/shard_map/psum | solution.py:152
  203.3 2.8 convolution_multiply_fusion
  206.2 2.3 convolution_multiply_fusion.1
  208.6 57.5 %reduce-scatter.3.cloned.1.call-done = f32[32,768]{1,0:T(8,128)} async-done(((f32[256,768]{1,0:T(8,128)}), f32[32,768]{1,0:T(8,128)}) %reduce-scatter.3.cloned.1.call-update) | async-done | bytes 98320 | tf_op jit(solution)/shard_map/reduce_scatter | solution.py:162
  266.1 1.1 multiply_reduce_fusion.1
  267.2 4.5 fusion.57
  272.6 3.7 all-to-all-start.2
  279.9 43.0 %all-reduce.1 = (f32[]{:T(128)}, f32[]{:T(128)}) all-reduce(f32[]{:T(128)S(6)} %add.312, f32[]{:T(128)} %get-tuple-element.4), channel_id=1, replica_groups=mesh['grp'=4,'dev'=8] {'grp','dev'}, use_global_device_ids=true, to_apply=%region_15.16 | all-reduce | flops 2 | bytes 16 | tf_op jit(solution)/shard_map/psum | solution.py:170
  324.2 1.1 multiply_reduce_fusion
  325.3 1.6 subtract_divide_fusion
  327.0 2.3 fusion.63
  329.3 6.1 %fusion.12 = f32[28,128,768]{2,1,0:T(8,128)} fusion(bf16[28,32,128]{2,1,0:T(8,128)(2,1)S(1)} %bitcast_select_fusion.2, pred[28]{0:T(512)(128)(4,1)S(1)} %get-tuple-element.14, bf16[32,768]{1,0:T(8,128)(2,1)S(1)} %get-tuple-element.34), kind=kOutput, calls=%fused_computation.28 | convolution fusion | flops 176275456 | bytes 11288604 | tf_op jit(solution)/shard_map/tkc,kd->tcd/dot_general | solution.py:187
  335.3 1.3 broadcast_in_dim.214
  336.6 25.4 %scatter_fusion = f32[4,128,768]{2,1,0:T(8,128)} fusion(f32[4,128,768]{2,1,0:T(8,128)} %broadcast_in_dim.214, s32[28]{0:T(128)S(1)} %get-tuple-element.15, f32[28,128,768]{2,1,0:T(8,128)} %fusion.12), kind=kCustom, calls=%fused_computation.5 | custom fusion | flops 2752512 | bytes 33030256 | tf_op jit(solution)/shard_map/scatter-add | solution.py:190
  362.0 32.4 %all_gather.18 = bf16[256,768]{1,0:T(8,128)(2,1)S(1)} all-gather(bf16[32,768]{1,0:T(8,128)(2,1)S(1)} %get-tuple-element.34), channel_id=1, replica_groups=mesh['grp'=4,'dev'=8] {'dev'}, dimensions={0}, use_global_device_ids=true | all-gather | bytes 442368 | tf_op jit(solution)/shard_map/all_gather | solution.py:198
  394.5 3.8 all-to-all-start.3
  398.3 3.7 fusion.64
  402.0 1.5 all-reduce.5.cloned.1.call-done
  403.5 6.1 %bitcast_select_fusion = f32[16,128,768]{2,1,0:T(8,128)} fusion(f32[8,2,128,768]{3,2,1,0:T(8,128)} %fusion.64, pred[16]{0:T(512)(128)(4,1)S(1)} %broadcast_in_dim.216), kind=kLoop, calls=%fused_computation.9 | loop fusion | flops 1572864 | bytes 12582928 | tf_op jit(solution)/shard_map/jit(_where)/select_n | solution.py:46
  409.6 14.9 %scatter_fusion.1 = f32[4,128,768]{2,1,0:T(8,128)} fusion(f32[4,128,768]{2,1,0:T(8,128)} %scatter_fusion, s32[16]{0:T(128)S(1)} %fusion.47, f32[16,128,768]{2,1,0:T(8,128)} %bitcast_select_fusion), kind=kCustom, calls=%fused_computation.6 | custom fusion | flops 1572864 | bytes 18874432 | tf_op jit(solution)/shard_map/scatter-add | solution.py:46
  424.5 7.1 %all_gather.19 = bf16[128,768]{1,0:T(8,128)(2,1)S(1)} all-gather(bf16[32,768]{1,0:T(8,128)(2,1)S(1)} %get-tuple-element.34), channel_id=1, replica_groups=mesh['grp'=4,'dev'=8] {'grp'}, dimensions={0}, use_global_device_ids=true | all-gather | bytes 245760 | tf_op jit(solution)/shard_map/all_gather | solution.py:214
  432.2 2.0 bitcast_select_fusion.1
  434.2 7.5 %scatter_fusion.2 = f32[4,128,768]{2,1,0:T(8,128)} fusion(f32[4,128,768]{2,1,0:T(8,128)} %scatter_fusion.1, s32[8]{0:T(128)S(1)} %fusion.48, f32[8,128,768]{2,1,0:T(8,128)} %bitcast_select_fusion.1), kind=kCustom, calls=%fused_computation.7 | custom fusion | flops 786432 | bytes 9437216 | tf_op jit(solution)/shard_map/scatter-add | solution.py:46
  441.7 3.5 scatter_fusion.3
  445.3 17.0 %all-reduce.7.cloned.1.call-done = f32[768,768]{1,0:T(8,128)} async-done(((f32[768,768]{1,0:T(8,128)}), f32[768,768]{1,0:T(8,128)}) %all-reduce.7.cloned.1.call-update) | async-done | bytes 2359312 | tf_op jit(solution)/shard_map/psum | solution.py:182
  462.3 3.2 copy.44
  (95 shorter events, 8.5 us)
Async XLA Ops:
  7.2 135.0 %copy-start = (f32[768,768]{1,0:T(8,128)S(1)}, f32[768,768]{1,0:T(8,128)}, u32[]{:S(2)}) copy-start(f32[768,768]{1,0:T(8,128)} %param.10) | copy-start | bytes 7077892
  15.3 25.1 %all-to-all-start.1 = ((bf16[4,2,128,768]{3,2,1,0:T(8,128)(2,1)}), bf16[4,2,128,768]{3,2,1,0:T(8,128)(2,1)}, u32[]{:S(2)}, u32[]{:S(2)}) async-start(bf16[4,2,128,768]{3,2,1,0:T(8,128)(2,1)} %select_select_fusion.1), calls=%async_computation.1 | async-start | bytes 3145728 | tf_op jit(solution)/shard_map/all_to_all | solution.py:113
  27.9 19.4 %copy-start.7 = (s32[32]{0:T(128)S(1)}, s32[32]{0:T(128)}, u32[]{:S(2)}) copy-start(s32[32]{0:T(128)} %param.12) | copy-start | bytes 388
  27.9 21.5 %copy-start.9 = (u32[32]{0:T(128)S(1)}, u32[32]{0:T(128)}, u32[]{:S(2)}) copy-start(u32[32]{0:T(128)} %constant.215) | copy-start | bytes 388
  27.9 25.5 %copy-start.8 = (s32[32]{0:T(128)S(1)}, s32[32]{0:T(128)}, u32[]{:S(2)}) copy-start(s32[32]{0:T(128)} %param.13) | copy-start | bytes 388
  27.9 90.8 %copy-start.3 = (f32[32,768]{1,0:T(8,128)S(1)}, f32[32,768]{1,0:T(8,128)}, u32[]{:S(2)}) copy-start(f32[32,768]{1,0:T(8,128)} %param.11) | copy-start | bytes 294916
  40.4 86.4 %all-to-all-start = ((bf16[8,2,128,768]{3,2,1,0:T(8,128)(2,1)}), bf16[8,2,128,768]{3,2,1,0:T(8,128)(2,1)}, u32[]{:S(2)}, u32[]{:S(2)}) async-start(bf16[8,2,128,768]{3,2,1,0:T(8,128)(2,1)} %select_select_fusion), calls=%async_computation | async-start | bytes 6291456 | tf_op jit(solution)/shard_map/all_to_all | solution.py:105
  47.1 219.0 %reduce-scatter.3.cloned.1.call-start = ((), (), s32[]{:S(2)}) async-start(), calls=%async_computation.6 | async-start | bytes 884736 | tf_op jit(solution)/shard_map/reduce_scatter | solution.py:162
  142.2 35.8 %copy-start.6 = (f32[32,768]{1,0:T(8,128)}, f32[32,768]{1,0:T(8,128)S(1)}, u32[]{:S(2)}) copy-start(f32[32,768]{1,0:T(8,128)S(1)} %fusion.7) | copy-start | bytes 294916
  142.2 33.8 %copy-start.2 = (f32[128,768]{1,0:T(8,128)S(1)}, f32[128,768]{1,0:T(8,128)}, u32[]{:S(2)}) copy-start(f32[128,768]{1,0:T(8,128)} %all_gather.16) | copy-start | bytes 1179652
  206.1 118.1 %reduce-scatter.5.cloned.1.call-start = ((), (), s32[]{:S(2)}) async-start(), calls=%async_computation.9 | async-start | bytes 491520 | tf_op jit(solution)/shard_map/reduce_scatter | solution.py:166
  208.5 194.9 %all-reduce.5.cloned.1.call-start = ((), (), s32[]{:S(2)}) async-start(), calls=%async_computation.7 | async-start | bytes 4718592 | tf_op jit(solution)/shard_map/psum | solution.py:182
  267.2 57.1 %copy-start.4 = (f32[32,768]{1,0:T(8,128)S(1)}, f32[32,768]{1,0:T(8,128)}, u32[]{:S(2)}) copy-start(f32[32,768]{1,0:T(8,128)} %param.11) | copy-start | bytes 294916
  267.2 59.8 %copy-start.5 = (f32[32,768]{1,0:T(8,128)S(1)}, f32[32,768]{1,0:T(8,128)}, u32[]{:S(2)}) copy-start(f32[32,768]{1,0:T(8,128)} %reduce-scatter.3.cloned.1.call-done) | copy-start | bytes 294916
  272.6 121.9 %all-to-all-start.2 = ((bf16[8,2,32,128]{3,2,1,0:T(8,128)(2,1)}), bf16[8,2,32,128]{3,2,1,0:T(8,128)(2,1)S(1)}, u32[]{:S(2)}, u32[]{:S(2)}) async-start(bf16[8,2,32,128]{3,2,1,0:T(8,128)(2,1)} %copy.27), calls=%async_computation.3 | async-start | bytes 262144 | tf_op jit(solution)/shard_map/all_to_all | solution.py:191
  394.5 37.1 %all-to-all-start.3 = ((bf16[4,2,32,128]{3,2,1,0:T(8,128)(2,1)}), bf16[4,2,32,128]{3,2,1,0:T(8,128)(2,1)S(1)}, u32[]{:S(2)}, u32[]{:S(2)}) async-start(bf16[4,2,32,128]{3,2,1,0:T(8,128)(2,1)} %copy.30), calls=%async_computation.4 | async-start | bytes 131072 | tf_op jit(solution)/shard_map/all_to_all | solution.py:207
  398.3 64.0 %all-reduce.7.cloned.1.call-start = ((), (), s32[]{:S(2)}) async-start(), calls=%async_computation.8 | async-start | bytes 4718592 | tf_op jit(solution)/shard_map/psum | solution.py:182
  441.7 23.8 %copy-start.1 = (f32[768,768]{1,0:T(8,128)S(1)}, f32[768,768]{1,0:T(8,128)}, u32[]{:S(2)}) copy-start(f32[768,768]{1,0:T(8,128)} %param.10) | copy-start | bytes 7077892
Sparse Core Ops, SparseCore 0:
  206.2 59.8 reduce-scatter.2
  268.6 20.0 reduce-scatter.4
  292.9 110.5 all-reduce.4
  405.7 56.5 all-reduce.6
